TPU v7x, 16 devices: a whole 2x2x2 slice. The times are simulated.
16 devices in a mesh: dp: 4 (over z, y), sp: 4 (over x, core).
Axes of the slice: x: 2, y: 2, z: 2, core: 2. Of those that a mesh axis runs over, the one named last changes fastest.
Arguments:
- tokens: bfloat16 [32768, 384], P(('dp', 'sp')), parts along dimension 0
- grad_out: bfloat16 [32768, 384], P(('dp', 'sp')), parts along dimension 0
- ln_gain: float32 [384], replicated
- ln_bias: float32 [384], replicated
- w_qkv: bfloat16 [384, 1152], replicated
- w_out: bfloat16 [384, 384], replicated
- temperature: float32 [8], replicated
Outputs:
- output 1: bfloat16 [32768, 384], P(('dp', 'sp')), parts along dimension 0
- output 2: bfloat16 [32768, 384], P(('dp', 'sp')), parts along dimension 0
- output 3: float32 [1536, 1152], P(('dp', 'sp')), parts along dimension 0
- output 4: float32 [1536, 384], P(('dp', 'sp')), parts along dimension 0
- output 5: float32 [1536], P('dp'), parts along dimension 0
- output 6: float32 [1536], P('dp'), parts along dimension 0
- output 7: float32 [32], P('dp'), parts along dimension 0
There are 4 independent parts. A program takes and returns all parts, laid end to end along the dimension named above; an argument that names none is the same for every part.
All inputs are finite; a program needn't handle non-finite values.
Results may differ from a plain program's by a relative error of at most 0.00130225.
Values are sent between devices in bfloat16 or wider.
A program may use at most 1 GiB of HBM per device.

v0:
```python
import jax
import jax.numpy as jnp
from jax import lax
from jax.sharding import PartitionSpec as P


def layer_norm(x_f32, ln_gain, ln_bias):
    row_mean = jnp.mean(x_f32, axis=-1, keepdims=True)
    centered = x_f32 - row_mean
    row_var = jnp.mean(centered * centered, axis=-1, keepdims=True)
    return centered * lax.rsqrt(row_var + 1e-6) * ln_gain + ln_bias


def attn_probs(gram_sum, q_sq, k_sq, value_a11):
    cosine = gram_sum / (jnp.sqrt(q_sq)[..., :, None] * jnp.sqrt(k_sq)[..., None, :])
    return jax.nn.softmax(value_a11[..., None, None] * cosine, axis=-1)


def project(x_rows, ln_gain, ln_bias, w_qkv, num_heads):
    ln_value, ln_vjp = jax.vjp(layer_norm, x_rows.astype(jnp.float32), ln_gain, ln_bias)
    normed = ln_value.astype(jnp.bfloat16)
    qkv_act = jnp.dot(normed, w_qkv, preferred_element_type=jnp.float32).astype(jnp.bfloat16)
    qkv_heads = qkv_act.reshape(x_rows.shape[0], 3, num_heads, -1)
    return ln_vjp, normed, qkv_heads[:, 0], qkv_heads[:, 1], qkv_heads[:, 2]


def apply_attn(v_heads, attn_weights):
    attn_out = jnp.einsum('nhj,hij->nhi', v_heads, attn_weights, preferred_element_type=jnp.float32)
    return attn_out.astype(jnp.bfloat16).reshape(v_heads.shape[0], -1)


def solution(mesh):
    row_spec = P(('dp', 'sp'), None)
    part_spec = P('dp')
    full_spec = P()

    def local_step(x_loc, dy_loc, ln_gain, ln_bias, w_qkv, w_out, value_a11):
        local_rows, model_width = x_loc.shape
        num_heads = value_a11.shape[0]
        fwd_act = project(x_loc, ln_gain, ln_bias, w_qkv, num_heads)
        q_heads, k_heads, v_heads = fwd_act[2], fwd_act[3], fwd_act[4]
        gram_part = jnp.einsum('nhi,nhj->hij', q_heads, k_heads, preferred_element_type=jnp.float32)
        qsq_part = jnp.einsum('nhi,nhi->hi', q_heads, q_heads, preferred_element_type=jnp.float32)
        ksq_part = jnp.einsum('nhj,nhj->hj', k_heads, k_heads, preferred_element_type=jnp.float32)
        gram_sum, q_sq, k_sq = lax.psum((gram_part, qsq_part, ksq_part), 'sp')
        attn_weights = attn_probs(gram_sum, q_sq, k_sq, value_a11).astype(jnp.bfloat16)
        attn_out = apply_attn(v_heads, attn_weights)
        out_proj = jnp.dot(attn_out, w_out, preferred_element_type=jnp.float32)
        out_tokens = (x_loc.astype(jnp.float32) + out_proj).astype(jnp.bfloat16)

        x_again, gram_kept, qsq_kept, ksq_kept = lax.optimization_barrier((x_loc, gram_sum, q_sq, k_sq))
        ln_vjp, normed, q_heads, k_heads, v_heads = project(x_again, ln_gain, ln_bias, w_qkv, num_heads)
        attn_f32, probs_vjp = jax.vjp(attn_probs, gram_kept, qsq_kept, ksq_kept, value_a11)
        attn_weights = attn_f32.astype(jnp.bfloat16)
        attn_out = apply_attn(v_heads, attn_weights)
        wout_part = jnp.einsum('nc,nd->cd', attn_out, dy_loc, preferred_element_type=jnp.float32)
        grad_w_out = lax.psum_scatter(wout_part, 'sp', scatter_dimension=0, tiled=True)
        d_attn = jnp.einsum('nd,cd->nc', dy_loc, w_out, preferred_element_type=jnp.float32)
        d_attn = d_attn.astype(jnp.bfloat16).reshape(local_rows, num_heads, -1)
        probs_part = jnp.einsum('nhi,nhj->hij', d_attn, v_heads, preferred_element_type=jnp.float32)
        d_probs = lax.psum(probs_part, 'sp')
        d_gram, d_qsq, d_ksq, value_a16 = probs_vjp(d_probs)
        d_gram_bf = d_gram.astype(jnp.bfloat16)
        d_q = jnp.einsum('hij,nhj->nhi', d_gram_bf, k_heads, preferred_element_type=jnp.float32) + 2.0 * q_heads * d_qsq
        d_k = jnp.einsum('hij,nhi->nhj', d_gram_bf, q_heads, preferred_element_type=jnp.float32) + 2.0 * k_heads * d_ksq
        d_v = jnp.einsum('hij,nhi->nhj', attn_weights, d_attn, preferred_element_type=jnp.float32)
        d_qkv = jnp.stack([d_q, d_k, d_v], axis=1).astype(jnp.bfloat16).reshape(local_rows, 3 * model_width)
        wqkv_part = jnp.einsum('nc,nk->ck', normed, d_qkv, preferred_element_type=jnp.float32)
        grad_w_qkv = lax.psum_scatter(wqkv_part, 'sp', scatter_dimension=0, tiled=True)
        d_normed = jnp.einsum('nk,ck->nc', d_qkv, w_qkv, preferred_element_type=jnp.float32)
        d_x, gain_part, bias_part = ln_vjp(d_normed)
        grad_gain, grad_bias = lax.psum((gain_part, bias_part), 'sp')
        grad_tokens = (dy_loc.astype(jnp.float32) + d_x).astype(jnp.bfloat16)
        return out_tokens, grad_tokens, grad_w_qkv, grad_w_out, grad_gain, grad_bias, value_a16

    return jax.shard_map(local_step, mesh=mesh,
                         in_specs=(row_spec, row_spec, full_spec, full_spec, full_spec, full_spec, full_spec),
                         out_specs=(row_spec, row_spec, row_spec, row_spec, part_spec, part_spec, part_spec),
                         check_vma=False)
```

profile of v0, /device:TPU:0, one launch (start us, length us, event | category | flops | bytes accessed | tf_op | source)
XLA Modules:
  0.0 149.3 jit_solution(14340552375036784229)
XLA Ops:
  7.3 1.9 %convert_reduce_fusion = f32[2048]{0:T(1024)S(1)} fusion(bf16[2048,384]{1,0:T(8,128)(2,1)} %param.7), kind=kLoop, calls=%fused_computation.7 | loop fusion | flops 1570816 | bytes 1581056 | tf_op jit(solution)/shard_map/jvp()/reduce_sum | solution.py:8
  9.2 2.2 %fusion.13 = f32[2048]{0:T(1024)S(1)} fusion(bf16[2048,384]{1,0:T(8,128)(2,1)} %param.7, f32[2048]{0:T(1024)S(1)} %broadcast_multiply_fusion.1), kind=kLoop, calls=%fused_computation.22 | loop fusion | flops 3143680 | bytes 1589248 | tf_op jit(solution)/shard_map/jvp()/reduce_sum | solution.py:10
  11.4 3.4 %convolution_convert_fusion.1 = bf16[2048,1152]{0,1:T(8,128)(2,1)S(1)} fusion(bf16[384,1152]{1,0:T(8,128)(2,1)S(1)} %copy-done, bf16[2048,384]{1,0:T(8,128)(2,1)S(1)} %copy-done.1, f32[384]{0:T(512)S(1)} %copy-done.12, f32[384]{0:T(512)S(1)} %copy-done.10, f32[2048]{0:T(1024)S(1)} %add_rsqrt_fusion, f32[2048]{0:T(1024)S(1)} %broadcast_multiply_fusion.1), kind=kOutput, calls=%fused_computation.3 | convolution fusion | flops 1819017216 | bytes 7195648 | tf_op jit(solution)/shard_map/dot_general | solution.py:22
  14.8 2.1 %copy-done.4 = bf16[2048,1152]{0,1:T(8,128)(2,1)} copy-done((bf16[2048,1152]{0,1:T(8,128)(2,1)}, bf16[2048,1152]{0,1:T(8,128)(2,1)S(1)}, u32[]{:S(2)}) %copy-start.4) | copy-done | bytes 4718616
  16.9 1.2 fusion.28
  18.3 3.7 %convolution_convert_fusion.4 = bf16[2048,384]{0,1:T(8,128)(2,1)} fusion(bf16[2048,384]{1,0:T(8,128)(2,1)} %param.8, bf16[384,384]{1,0:T(8,128)(2,1)S(1)} %copy-done.9), kind=kOutput, calls=%fused_computation.40 | convolution fusion | flops 604766208 | bytes 3440640 | tf_op jit(solution)/shard_map/nd,cd->nc/dot_general | solution.py:58
  22.7 8.9 %all-reduce.1 = (f32[8,48]{1,0:T(8,128)S(1)}, f32[8,48]{1,0:T(8,128)S(1)}) all-reduce(f32[8,48]{1,0:T(8,128)S(1)} %get-tuple-element.18, f32[8,48]{1,0:T(8,128)S(1)} %get-tuple-element.17), channel_id=1, replica_groups=mesh['dp'=4,'sp'=4] {'sp'}, use_global_device_ids=true, to_apply=%region_4.0 | all-reduce | flops 768 | bytes 6144 | tf_op jit(solution)/shard_map/psum | solution.py:45
  31.6 17.8 %all-reduce.5.cloned.1.call-done = f32[8,48,48]{2,1,0:T(8,128)} async-done(((f32[8,48,48]{2,1,0:T(8,128)}), f32[8,48,48]{2,1,0:T(8,128)}) %all-reduce.5.cloned.1.call-update) | async-done | bytes 73744 | tf_op jit(solution)/shard_map/psum | solution.py:45
  49.8 0.8 fusion.17
  50.6 2.0 %fusion.69 = (f32[8,48]{1,0:T(8,128)S(1)}, f32[8,48,48]{2,1,0:T(8,128)S(1)}) fusion(f32[8]{0:T(128)S(1)} %copy-done.11, f32[8,48,48]{2,1,0:T(8,128)S(1)} %copy-done.8, f32[8,48]{1,0:T(8,128)S(1)} %sqrt.15, f32[8,48]{1,0:T(8,128)S(1)} %sqrt.14), kind=kOutput, calls=%fused_computation.99 | output fusion | flops 92207 | bytes 152096 | tf_op jit(solution)/shard_map/jvp()/sub | solution.py:16
  52.6 4.9 %convolution_convert_fusion = bf16[2048,1152]{0,1:T(8,128)(2,1)} fusion(bf16[384,1152]{1,0:T(8,128)(2,1)S(1)} %copy-done, bf16[2048,384]{1,0:T(8,128)(2,1)S(1)} %copy-done.1, f32[2048]{0:T(1024)S(1)} %fusion.50, f32[2048]{0:T(1024)S(1)} %broadcast_multiply_fusion, f32[384]{0:T(512)S(1)} %copy-done.12, f32[384]{0:T(512)S(1)} %copy-done.10), kind=kOutput, calls=%fused_computation.2 | convolution fusion | flops 1819017216 | bytes 7195648 | tf_op jit(solution)/shard_map/dot_general | solution.py:22
  57.5 4.0 %convolution_convert_fusion.2 = bf16[8,48,2048]{2,1,0:T(8,128)(2,1)} fusion(bf16[2048,3,8,48]{0,3,2,1:T(8,128)(2,1)} %bitcast.85, f32[8,48]{1,0:T(8,128)S(1)} %get-tuple-element.30, f32[8]{0:T(128)S(1)} %copy-done.11, f32[8,48,48]{2,1,0:T(8,128)S(1)} %copy-done.8, f32[8,48]{1,0:T(8,128)S(1)} %sqrt.15, f32[8,48]{1,0:T(8,128)S(1)} %sqrt.14), kind=kOutput, calls=%fused_computation.38 | convolution fusion | flops 76394928 | bytes 3224096 | tf_op jit(solution)/shard_map/nhj,hij->nhi/dot_general | solution.py:28
  61.5 3.1 %fusion.35 = f32[8,48,48]{2,1,0:T(8,128)} fusion(bf16[2048,8,48]{0,2,1:T(8,128)(2,1)} %bitcast.76, bf16[2048,3,8,48]{0,3,2,1:T(8,128)(2,1)} %bitcast.86), kind=kOutput, calls=%fused_computation.56 | convolution fusion | flops 75497472 | bytes 3219456 | tf_op jit(solution)/shard_map/nhi,nhj->hij/dot_general | solution.py:60
  64.7 3.7 %fusion.70 = f32[384,384]{1,0:T(8,128)} fusion(bf16[2048,384]{0,1:T(8,128)(2,1)} %bitcast.83, bf16[2048,384]{1,0:T(8,128)(2,1)} %param.8), kind=kOutput, calls=%fused_computation.100 | convolution fusion | flops 603979776 | bytes 3735552 | tf_op jit(solution)/shard_map/nc,nd->cd/dot_general | solution.py:56
  68.4 4.2 %fusion.24 = bf16[2048,1,8,48]{0,3,2,1:T(8,128)(2,1)} fusion(bf16[2048,8,48]{0,2,1:T(8,128)(2,1)} %bitcast.77, f32[8,48]{1,0:T(8,128)S(1)} %get-tuple-element.30, f32[8]{0:T(128)S(1)} %copy-done.11, f32[8,48,48]{2,1,0:T(8,128)S(1)} %copy-done.8, f32[8,48]{1,0:T(8,128)S(1)} %sqrt.15, f32[8,48]{1,0:T(8,128)S(1)} %sqrt.14), kind=kOutput, calls=%fused_computation.42 | convolution fusion | flops 76394928 | bytes 3224096 | tf_op jit(solution)/shard_map/hij,nhi->nhj/dot_general | solution.py:66
  72.9 20.1 %all-reduce.7.cloned.1.call-done = f32[8,48,48]{2,1,0:T(8,128)} async-done(((f32[8,48,48]{2,1,0:T(8,128)}), f32[8,48,48]{2,1,0:T(8,128)}) %all-reduce.7.cloned.1.call-update) | async-done | bytes 73744 | tf_op jit(solution)/shard_map/psum | solution.py:61
  93.0 1.2 multiply_reduce_fusion.3
  94.2 1.2 fusion.46
  95.3 0.8 multiply_reduce_fusion.2
  96.1 2.9 %fusion.26 = bf16[2048,1,8,48]{0,3,2,1:T(8,128)(2,1)S(1)} fusion(f32[8,48]{1,0:T(8,128)S(1)} %get-tuple-element.33, bf16[2048,3,8,48]{0,3,2,1:T(8,128)(2,1)} %bitcast.87, f32[8,48,48]{2,1,0:T(8,128)S(1)} %get-tuple-element.29, f32[8,48]{1,0:T(8,128)S(1)} %sqrt.15, f32[8,48]{1,0:T(8,128)S(1)} %sqrt.14, f32[8]{0:T(128)S(1)} %copy-done.11), kind=kOutput, calls=%fused_computation.44 | convolution fusion | flops 79503360 | bytes 4796960 | tf_op jit(solution)/shard_map/hij,nhi->nhj/dot_general | solution.py:65
  99.1 2.8 %fusion.25 = bf16[2048,1,8,48]{0,3,2,1:T(8,128)(2,1)S(1)} fusion(f32[8,48]{1,0:T(8,128)S(1)} %get-tuple-element.34, bf16[2048,3,8,48]{0,3,2,1:T(8,128)(2,1)} %bitcast.88, f32[8,48,48]{2,1,0:T(8,128)S(1)} %get-tuple-element.29, f32[8,48]{1,0:T(8,128)S(1)} %sqrt.15, f32[8,48]{1,0:T(8,128)S(1)} %sqrt.14, f32[8]{0:T(128)S(1)} %copy-done.11), kind=kOutput, calls=%fused_computation.43 | convolution fusion | flops 79503360 | bytes 4796960 | tf_op jit(solution)/shard_map/hij,nhj->nhi/dot_general | solution.py:64
  102.4 2.2 %copy-done.6 = bf16[2048,3,8,48]{0,3,2,1:T(8,128)(2,1)} copy-done((bf16[2048,3,8,48]{0,3,2,1:T(8,128)(2,1)}, bf16[2048,3,8,48]{0,3,2,1:T(8,128)(2,1)S(1)}, u32[]{:S(2)}) %copy-start.6) | copy-done | bytes 4718616
  104.6 4.1 %fusion.63 = f32[384,1152]{1,0:T(8,128)} fusion(bf16[2048,1152]{0,1:T(8,128)(2,1)S(1)} %bitcast.81, bf16[2048,384]{1,0:T(8,128)(2,1)S(1)} %copy-done.1, f32[2048]{0:T(1024)S(1)} %fusion.50, f32[2048]{0:T(1024)S(1)} %broadcast_multiply_fusion, f32[384]{0:T(512)S(1)} %copy-done.12, f32[384]{0:T(512)S(1)} %copy-done.10), kind=kOutput, calls=%fused_computation.95 | convolution fusion | flops 1816657920 | bytes 8080384 | tf_op jit(solution)/shard_map/nc,nk->ck/dot_general | solution.py:68
  108.8 1.5 %fusion.68 = f32[8,48]{1,0:T(8,128)S(1)} fusion(f32[8,48,48]{2,1,0:T(8,128)S(1)} %copy-done.8, f32[8,48]{1,0:T(8,128)S(1)} %sqrt.13, f32[8,48]{1,0:T(8,128)S(1)} %sqrt.12, f32[8]{0:T(128)S(1)} %copy-done.11), kind=kOutput, calls=%fused_computation.98 | output fusion | flops 92207 | bytes 78368 | tf_op jit(solution)/shard_map/sub | solution.py:16
  110.3 4.0 %convolution_convert_fusion.5 = bf16[8,48,2048]{2,1,0:T(8,128)(2,1)} fusion(bf16[2048,3,8,48]{0,3,2,1:T(8,128)(2,1)} %bitcast.79, f32[8,48]{1,0:T(8,128)S(1)} %fusion.68, f32[8,48,48]{2,1,0:T(8,128)S(1)} %copy-done.8, f32[8,48]{1,0:T(8,128)S(1)} %sqrt.13, f32[8,48]{1,0:T(8,128)S(1)} %sqrt.12, f32[8]{0:T(128)S(1)} %copy-done.11), kind=kOutput, calls=%fused_computation.41 | convolution fusion | flops 76394928 | bytes 3224096 | tf_op jit(solution)/shard_map/nhj,hij->nhi/dot_general | solution.py:28
  114.4 3.9 %fusion.19 = bf16[2048,384]{1,0:T(8,128)(2,1)} fusion(bf16[2048,384]{1,0:T(8,128)(2,1)S(1)} %copy-done.1, bf16[2048,384]{0,1:T(8,128)(2,1)} %bitcast.84, bf16[384,384]{1,0:T(8,128)(2,1)S(1)} %copy-done.9), kind=kOutput, calls=%fused_computation.28 | convolution fusion | flops 606339072 | bytes 5013504 | tf_op jit(solution)/shard_map/dot_general | solution.py:48
  118.2 3.8 %fusion.67 = (f32[384]{0:T(512)S(1)}, f32[2048]{0:T(1024)S(1)}, f32[2048,384]{1,0:T(8,128)S(1)}) fusion(f32[384]{0:T(512)S(1)} %copy-done.10, f32[2048]{0:T(1024)S(1)} %broadcast_multiply_fusion, bf16[2048,384]{1,0:T(8,128)(2,1)S(1)} %copy-done.1, bf16[2048,1152]{0,1:T(8,128)(2,1)S(1)} %bitcast.82, bf16[384,1152]{1,0:T(8,128)(2,1)S(1)} %copy-done), kind=kOutput, calls=%fused_computation.97 | convolution fusion | flops 1816655488 | bytes 10341376 | tf_op jit(solution)/shard_map/nk,ck->nc/dot_general | solution.py:70
  122.1 1.6 %copy-done.2 = f32[2048,384]{1,0:T(8,128)} copy-done((f32[2048,384]{1,0:T(8,128)}, f32[2048,384]{1,0:T(8,128)S(1)}, u32[]{:S(2)}) %copy-start.2) | copy-done | bytes 3145752
  123.7 1.6 %fusion.12 = (f32[384]{0:T(512)S(1)}, f32[2048]{0:T(1024)S(1)}) fusion(f32[2048,384]{1,0:T(8,128)S(1)} %get-tuple-element.32, bf16[2048,384]{1,0:T(8,128)(2,1)S(1)} %copy-done.1, f32[2048]{0:T(1024)S(1)} %fusion.50, f32[2048]{0:T(1024)S(1)} %broadcast_multiply_fusion, f32[2048]{0:T(1024)S(1)} %multiply_multiply_fusion.1, f32[384]{0:T(512)S(1)} %copy-done.10), kind=kLoop, calls=%fused_computation.21 | loop fusion | flops 8648320 | bytes 4754432 | tf_op jit(solution)/shard_map/transpose(jvp())/reduce_sum | solution.py:11
  125.3 6.3 %all-reduce = (f32[384]{0:T(512)}, f32[384]{0:T(512)}) all-reduce(f32[384]{0:T(512)S(1)} %get-tuple-element.15, f32[384]{0:T(512)S(1)} %get-tuple-element.19), channel_id=1, replica_groups=mesh['dp'=4,'sp'=4] {'sp'}, use_global_device_ids=true, to_apply=%region_20.0 | all-reduce | flops 768 | bytes 6144 | tf_op jit(solution)/shard_map/psum | solution.py:72
  131.7 5.0 %add_convert_fusion = bf16[2048,384]{1,0:T(8,128)(2,1)} fusion(bf16[2048,384]{1,0:T(8,128)(2,1)} %param.8, f32[2048]{0:T(1024)S(1)} %negate_multiply_fusion, f32[2048]{0:T(1024)S(1)} %multiply_multiply_fusion.1, f32[2048]{0:T(1024)S(1)} %broadcast_multiply_fusion, bf16[2048,384]{1,0:T(8,128)(2,1)S(1)} %copy-done.1, f32[2048]{0:T(1024)S(1)} %fusion.50, ...), kind=kLoop, calls=%fused_computation.37 | loop fusion | flops 8650752 | bytes 7898624 | tf_op jit(solution)/shard_map/convert_element_type | solution.py:73
  136.7 6.1 %reduce-scatter.3.cloned.1.call-done = f32[96,1152]{1,0:T(8,128)} async-done(((f32[384,1152]{1,0:T(8,128)}), f32[96,1152]{1,0:T(8,128)}) %reduce-scatter.3.cloned.1.call-update) | async-done | bytes 442384 | tf_op jit(solution)/shard_map/reduce_scatter | solution.py:69
  (48 shorter events, 2.1 us)
Async XLA Ops:
  7.2 4.2 %copy-start = (bf16[384,1152]{1,0:T(8,128)(2,1)S(1)}, bf16[384,1152]{1,0:T(8,128)(2,1)}, u32[]{:S(2)}) copy-start(bf16[384,1152]{1,0:T(8,128)(2,1)} %param.11) | copy-start | bytes 2654212
  7.2 4.2 %copy-start.1 = (bf16[2048,384]{1,0:T(8,128)(2,1)S(1)}, bf16[2048,384]{1,0:T(8,128)(2,1)}, u32[]{:S(2)}) copy-start(bf16[2048,384]{1,0:T(8,128)(2,1)} %param.7) | copy-start | bytes 4718596
  7.2 4.2 %copy-start.10 = (f32[384]{0:T(512)S(1)}, f32[384]{0:T(512)}, u32[]{:S(2)}) copy-start(f32[384]{0:T(512)} %param.9) | copy-start | bytes 4612
  7.2 4.2 %copy-start.12 = (f32[384]{0:T(512)S(1)}, f32[384]{0:T(512)}, u32[]{:S(2)}) copy-start(f32[384]{0:T(512)} %param.10) | copy-start | bytes 4612
  7.2 42.2 %all-reduce.5.cloned.1.call-start = ((), (), s32[]{:S(2)}) async-start(), calls=%async_computation.2 | async-start | bytes 393216 | tf_op jit(solution)/shard_map/psum | solution.py:45
  14.8 2.1 %copy-start.4 = (bf16[2048,1152]{0,1:T(8,128)(2,1)}, bf16[2048,1152]{0,1:T(8,128)(2,1)S(1)}, u32[]{:S(2)}) copy-start(bf16[2048,1152]{0,1:T(8,128)(2,1)S(1)} %convolution_convert_fusion.1) | copy-start | bytes 14155780
  14.8 3.4 %copy-start.9 = (bf16[384,384]{1,0:T(8,128)(2,1)S(1)}, bf16[384,384]{1,0:T(8,128)(2,1)}, u32[]{:S(2)}) copy-start(bf16[384,384]{1,0:T(8,128)(2,1)} %param.12) | copy-start | bytes 884740
  18.2 74.8 %all-reduce.7.cloned.1.call-start = ((), (), s32[]{:S(2)}) async-start(), calls=%async_computation.3 | async-start | bytes 393216 | tf_op jit(solution)/shard_map/psum | solution.py:61
  18.3 3.7 %copy-start.5 = (bf16[2048,1152]{0,1:T(8,128)(2,1)S(1)}, bf16[2048,1152]{0,1:T(8,128)(2,1)}, u32[]{:S(2)}) copy-start(bf16[2048,1152]{0,1:T(8,128)(2,1)} %copy-done.4) | copy-start | bytes 14155780
  22.0 28.6 %copy-start.11 = (f32[8]{0:T(128)S(1)}, f32[8]{0:T(128)}, u32[]{:S(2)}) copy-start(f32[8]{0:T(128)} %param.13) | copy-start | bytes 100
  49.4 1.2 copy-start.8
  64.7 72.0 %reduce-scatter.5.cloned.1.call-start = ((), (), s32[]{:S(2)}) async-start(), calls=%async_computation.5 | async-start | bytes 737280 | tf_op jit(solution)/shard_map/reduce_scatter | solution.py:57
  72.6 70.1 %reduce-scatter.3.cloned.1.call-start = ((), (), s32[]{:S(2)}) async-start(), calls=%async_computation.4 | async-start | bytes 2211840 | tf_op jit(solution)/shard_map/reduce_scatter | solution.py:69
  99.1 2.8 %copy-start.3 = (bf16[2048,1,8,48]{0,3,2,1:T(8,128)(2,1)S(1)}, bf16[2048,1,8,48]{0,3,2,1:T(8,128)(2,1)}, u32[]{:S(2)}) copy-start(bf16[2048,1,8,48]{0,3,2,1:T(8,128)(2,1)} %fusion.24) | copy-start | bytes 4718596
  102.4 2.2 %copy-start.6 = (bf16[2048,3,8,48]{0,3,2,1:T(8,128)(2,1)}, bf16[2048,3,8,48]{0,3,2,1:T(8,128)(2,1)S(1)}, u32[]{:S(2)}) copy-start(bf16[2048,3,8,48]{0,3,2,1:T(8,128)(2,1)S(1)} %pad_maximum_fusion) | copy-start | bytes 14155780
  114.4 3.9 %copy-start.7 = (bf16[2048,3,8,48]{0,3,2,1:T(8,128)(2,1)S(1)}, bf16[2048,3,8,48]{0,3,2,1:T(8,128)(2,1)}, u32[]{:S(2)}) copy-start(bf16[2048,3,8,48]{0,3,2,1:T(8,128)(2,1)} %copy-done.6) | copy-start | bytes 14155780
  122.0 1.7 %copy-start.2 = (f32[2048,384]{1,0:T(8,128)}, f32[2048,384]{1,0:T(8,128)S(1)}, u32[]{:S(2)}) copy-start(f32[2048,384]{1,0:T(8,128)S(1)} %get-tuple-element.32) | copy-start | bytes 9437188
Sparse Core Ops, SparseCore 0:
  18.3 31.0 all-reduce.4
  64.8 28.1 all-reduce.6
  96.1 18.2 reduce-scatter.4
  117.3 25.3 reduce-scatter.2
where the time goes:
time: 150 us; the launch traced here: 149 us
  matrix products  49.8 us (33%)
  waiting for transfers between devices  44.1 us (29%)
  other arithmetic  19.8 us (13%)
  blocking collectives  15.2 us (10%)
  between operations  14.1 us (9%)
  local copies, waits for them, and re-layouts  5.98 us (4%)
    psum x1, waiting for transfers between devices, local_step(): d_probs = lax.psum(probs_part, 'sp')  20.1 us
    psum x1, waiting for transfers between devices, local_step(): gram_sum, q_sq, k_sq = lax.psum((gram_part, qsq_part, ksq_part), 'sp')  17.8 us
    psum x1, blocking collectives, local_step(): gram_sum, q_sq, k_sq = lax.psum((gram_part, qsq_part, ksq_part), 'sp')  8.9 us
    dot_general x2, matrix products, project(): jnp.dot(normed, w_qkv, preferred_element_type=jnp.float32)  8.22 us
    dot_general x2, matrix products, apply_attn(): jnp.einsum('nhj,hij->nhi', v_heads, attn_weights, preferred_element_type=...  8.08 us
    psum x1, blocking collectives, local_step(): grad_gain, grad_bias = lax.psum((gain_part, bias_part), 'sp')  6.34 us
    reduce_scatter x1, waiting for transfers between devices, local_step(): lax.psum_scatter(wqkv_part, 'sp', scatter_dimension=0, tiled=True)  6.08 us
    unnamed x26, local copies, waits for them, and re-layouts  5.96 us
  transfers between devices with their start and end apart: 4, of which 3 were waited for; matrix products, arithmetic and copies ran while one was open for 31% of the time, Pallas kernels for 0%

commit v1 on v0

v1 whole, which is shorter than its diff:
```python
import jax
import jax.numpy as jnp
from jax import lax
from jax.experimental import pallas as pl
from jax.experimental.pallas import tpu as pltpu
from jax.sharding import PartitionSpec as P

F32 = jnp.float32
BF16 = jnp.bfloat16
MESH = pl.DeviceIdType.MESH
C = 384
GC = 192
HD = 48
NT = 2048
BLK = 256
NB = NT // BLK
EPS = 1e-6

S_GRAM, S_DPROB, S_ATTN, S_DGRAM, S_DSQ = 0, 3, 6, 7, 8
S_GWO, S_GWV, S_GWQK, S_LN = 9, 12, 15, 18
N_SEM = 21


def nn(a, b):
    return jnp.dot(a, b, preferred_element_type=F32)


def nt(a, b):
    return lax.dot_general(a, b, (((1,), (1,)), ((), ())), preferred_element_type=F32)


def transpose_bf16(a):
    return a.T


def lanes(shape):
    return lax.broadcasted_iota(jnp.int32, shape, len(shape) - 1)


def rows(shape):
    return lax.broadcasted_iota(jnp.int32, shape, 0)


def pack_heads(dense_ref, dst_ref, g, sq_col=None, sk_col=None):
    lane = lanes((HD, 128))
    for pair in range(2):
        total = jnp.zeros((HD, 128), F32)
        for side in range(2):
            h = 2 * pair + side
            r = pl.ds(HD * h, HD)
            block = dense_ref[g, r, :]
            block = pltpu.roll(block, (64 * side - HD * h) % 256, 1)[:, :128]
            base = 64 * side
            total = jnp.where((lane >= base) & (lane < base + HD), block, total)
            if sq_col is not None:
                rr = slice(HD * h, HD * h + HD)
                total = jnp.where(lane == base + HD, sq_col[rr], total)
                total = jnp.where(lane == base + HD + 1, sk_col[rr], total)
        dst_ref[g, pl.ds(HD * pair, HD), :] = total


def unpack_heads(packed):
    parts = []
    for pair in range(2):
        p = packed[HD * pair:HD * pair + HD]
        parts += [p, pltpu.roll(p, 64, 1)]
    return jnp.concatenate(parts, axis=0)


def spread_heads(compact):
    parts = []
    for h in range(4):
        block = compact[HD * h:HD * h + HD]
        block = jnp.concatenate([block, jnp.zeros((HD, 128), F32)], axis=1)
        parts.append(pltpu.roll(block, HD * h, 1) if h else block)
    return jnp.concatenate(parts, axis=0)


def col(x, lane, index):
    return jnp.sum(jnp.where(lane == index, x, 0.0), axis=1, keepdims=True)


def per_head_row(column):
    parts = []
    for h in range(4):
        part = jnp.broadcast_to(column[HD * h:HD * h + HD], (HD, 128))
        eye = rows((HD, 128)) == lanes((HD, 128))
        row = jnp.sum(jnp.where(eye, part, 0.0), axis=0, keepdims=True)
        parts.append(jnp.broadcast_to(row, (HD, 128)))
    return jnp.concatenate(parts, axis=0)


def per_head_sum_col(x):
    parts = []
    for h in range(4):
        row = jnp.sum(x[HD * h:HD * h + HD], axis=0, keepdims=True)
        eye = rows((HD, 128)) == lanes((HD, 128))
        parts.append(jnp.sum(jnp.where(eye, jnp.broadcast_to(row, (HD, 128)), 0.0), axis=1, keepdims=True))
    return jnp.concatenate(parts, axis=0)


def body(x_hbm, dy_hbm, gain_ref, bias_ref, wqkv_hbm, wout_hbm, temp_ref,
         out_hbm, gt_hbm, gwqkv_hbm, gwout_hbm, gg_ref, gb_ref, gtemp_ref,
         x_v, dy_v, w_v, wo_v, wT, woT, xT, dyT, uT, mean_v, rstd_v, qkvT, doT, oT, dqkvT, outR, gtR,
         gainB, biasB, ssq, gacc, dacc, gsend, grecv, dsend, drecv, lhsA, lhsAT, lhsD, lhsDT, dsq_v,
         Po, Pv, Pqk, Ro, Rv, Rqk, To, Tv, Tqk, Io, Iv, Iqk, lnsend, lnrecv, lnacc,
         ssem, rsem, dsem):
    s = lax.axis_index("sp")
    chip, core = s // 2, s % 2
    sib = chip * 2 + (1 - core)
    cp = (1 - chip) * 2 + core
    dg = (1 - chip) * 2 + (1 - core)
    other = 1 - core

    barrier = pltpu.get_barrier_semaphore()
    for dev in (sib, cp, dg):
        pl.semaphore_signal(barrier, inc=1, device_id={"sp": dev}, device_id_type=MESH)

    def remote(src, dst, i, dev):
        return pltpu.make_async_remote_copy(src_ref=src, dst_ref=dst, send_sem=ssem.at[i], recv_sem=rsem.at[i],
                                            device_id={"sp": dev}, device_id_type=MESH)

    def local(src, dst, i):
        return pltpu.make_async_copy(src, dst, dsem.at[i])

    nx = 4
    xr = NT // nx
    in_w = local(wqkv_hbm, w_v, 0)
    in_wo = local(wout_hbm, wo_v, 1)
    in_x = [local(x_hbm.at[pl.ds(i * xr, xr)], x_v.at[pl.ds(i * xr, xr)], 2 + i) for i in range(nx)]
    in_dy = [local(dy_hbm.at[pl.ds(i * xr, xr)], dy_v.at[pl.ds(i * xr, xr)], 6 + i) for i in range(nx)]
    in_x[0].start()
    in_w.start()
    for d in in_x[1:] + [in_wo] + in_dy:
        d.start()

    gainB[...] = jnp.broadcast_to(gain_ref[...], (128, C)).T
    biasB[...] = jnp.broadcast_to(bias_ref[...], (128, C)).T
    gacc[...] = jnp.zeros(gacc.shape, F32)
    dacc[...] = jnp.zeros(dacc.shape, F32)

    def wide(ref):
        v = ref[...]
        return jnp.concatenate([v] * (BLK // 128), axis=1)

    for b in range(NB):
        t = pl.ds(b * BLK, BLK)
        if (b * BLK) % xr == 0:
            in_x[b * BLK // xr].wait()
        xt = transpose_bf16(x_v[t, :])
        xT[:, t] = xt
        xf = xt.astype(F32)
        mean = jnp.sum(xf, axis=0, keepdims=True) * (1.0 / C)
        xc = xf - mean
        var = jnp.sum(xc * xc, axis=0, keepdims=True) * (1.0 / C)
        rstd = lax.rsqrt(var + EPS)
        mean_v[:, t] = mean
        rstd_v[:, t] = rstd
        u = (xc * rstd * wide(gainB) + wide(biasB)).astype(BF16)
        uT[:, t] = u
        if b == 0:
            in_w.wait()
            wT[...] = transpose_bf16(w_v[...])
        qk = nn(wT[pl.ds(0, 2 * C), :], u).astype(BF16)
        qkvT[pl.ds(0, 4), :, t] = qk.reshape(4, GC, BLK)
        qf = qk.astype(F32)
        sqr = qf * qf
        part = sqr[:, :128]
        for i in range(1, BLK // 128):
            part = part + sqr[:, 128 * i:128 * i + 128]
        ssq[...] = part if b == 0 else ssq[...] + part
        for g in range(2):
            gacc[g, :, pl.ds(0, GC)] += nt(qk[GC * g:GC * g + GC], qk[C + GC * g:C + GC * g + GC])

    sums = jnp.sum(ssq[...], axis=1, keepdims=True)
    for g in range(2):
        pack_heads(gacc, gsend, g, sums[GC * g:GC * g + GC], sums[C + GC * g:C + GC * g + GC])

    pl.semaphore_wait(barrier, 3)
    pending = []

    def send(src, dst, i, dev):
        d = remote(src, dst, i, dev)
        d.start()
        pending.append(d)
        return d

    gram_x = [send(gsend.at[core], grecv.at[1], S_GRAM + 1, cp),
              send(gsend.at[other], grecv.at[2], S_GRAM + 2, dg),
              send(gsend.at[other], grecv.at[0], S_GRAM, sib)]

    in_wo.wait()
    woT[...] = transpose_bf16(wo_v[...])
    for b in range(NB):
        t = pl.ds(b * BLK, BLK)
        if (b * BLK) % xr == 0:
            in_dy[b * BLK // xr].wait()
        v = nn(wT[pl.ds(2 * C, C), :], uT[:, t]).astype(BF16)
        qkvT[pl.ds(4, 2), :, t] = v.reshape(2, GC, BLK)
        dyt = transpose_bf16(dy_v[t, :])
        dyT[:, t] = dyt
        do = nn(wo_v[...], dyt).astype(BF16)
        doT[:, :, t] = do.reshape(2, GC, BLK)
        for g in range(2):
            dacc[g, :, pl.ds(0, GC)] += nt(do[GC * g:GC * g + GC], v[GC * g:GC * g + GC])
    for g in range(2):
        pack_heads(dacc, dsend, g)
    dprob_x = [send(dsend.at[core], drecv.at[1], S_DPROB + 1, cp),
               send(dsend.at[other], drecv.at[2], S_DPROB + 2, dg),
               send(dsend.at[other], drecv.at[0], S_DPROB, sib)]

    for d in gram_x:
        d.wait_recv()
    lane = lanes((GC, 128))
    valid = lane < HD
    head_row = rows((GC, 1))
    tcol = jnp.zeros((GC, 1), F32)
    for h in range(4):
        tcol = jnp.where((head_row >= HD * h) & (head_row < HD * h + HD), temp_ref[4 * core + h], tcol)
    gsum = unpack_heads((gsend[core] + grecv[0]) + (grecv[1] + grecv[2]))
    sq_c = col(gsum, lane, HD)
    sk_c = col(gsum, lane, HD + 1)
    nq = jnp.sqrt(sq_c)
    nk_c = jnp.sqrt(sk_c)
    nk = per_head_row(nk_c)
    den = jnp.where(valid, nq * nk, 1.0)
    cosine = jnp.where(valid, gsum / den, 0.0)
    logit = tcol * cosine
    top = jnp.max(jnp.where(valid, logit, -jnp.inf), axis=1, keepdims=True)
    e = jnp.where(valid, jnp.exp(logit - top), 0.0)
    attn = e / jnp.sum(e, axis=1, keepdims=True)
    lhsA[core] = spread_heads(attn).astype(BF16)
    attn_x = send(lhsA.at[core], lhsA.at[core], S_ATTN, sib)

    def transposed(src, dst, g):
        v = src[g]
        dst[g] = jnp.concatenate([v, jnp.zeros((64, 256), BF16)], axis=0).T[:GC]

    def reduce_send(P, R, i):
        send(P.at[sib], R.at[0], i, sib)
        send(P.at[dg], R.at[1], i + 1, sib)

    def reduce_next(P, R, T, I, i):
        remote(P.at[dg], R.at[1], i + 1, sib).wait_recv()
        T[...] = P[cp] + R[1]
        send(T, I, i + 2, cp)

    for step, g in enumerate((core, other)):
        if step == 1:
            remote(lhsA.at[other], lhsA.at[other], S_ATTN, sib).wait_recv()
        o = nn(lhsA[g][:, :GC], qkvT[4 + g])
        oT[g] = o.astype(BF16)
    Po[...] = nn(oT[...].reshape(C, NT), dy_v[...]).reshape(4, 96, C)
    reduce_send(Po, Ro, S_GWO)

    for g in range(2):
        transposed(lhsA, lhsAT, g)
        dqkvT[4 + g] = nn(lhsAT[g][:, :GC], doT[g]).astype(BF16)
    Pv[...] = nt(uT[...], dqkvT[pl.ds(4, 2)].reshape(C, NT)).reshape(4, 96, C)
    reduce_send(Pv, Rv, S_GWV)
    reduce_next(Po, Ro, To, Io, S_GWO)

    for d in dprob_x:
        d.wait_recv()
    dprob = unpack_heads((dsend[core] + drecv[0]) + (drecv[1] + drecv[2]))
    dprob = jnp.where(valid, dprob, 0.0)
    ds = attn * (dprob - jnp.sum(attn * dprob, axis=1, keepdims=True))
    dtrow = jnp.sum(ds * cosine, axis=1, keepdims=True)
    dcos = tcol * ds
    dc = dcos * cosine
    dgram = jnp.where(valid, dcos / den, 0.0)
    dsq = -0.5 * (jnp.sum(dc, axis=1, keepdims=True) / nq) / nq
    dsk = -0.5 * (per_head_sum_col(dc) / nk_c) / nk_c
    info = jnp.where(lane == 0, dsq, jnp.where(lane == 1, dsk, 0.0))
    for h in range(4):
        dt = jnp.sum(dtrow[HD * h:HD * h + HD], axis=0, keepdims=True)
        info = jnp.where((lane == 2 + h), dt, info)
    dsq_v[core] = info
    lhsD[core] = spread_heads(dgram).astype(BF16)
    send(lhsD.at[core], lhsD.at[core], S_DGRAM, sib)
    send(dsq_v.at[core], dsq_v.at[core], S_DSQ, sib)

    for step, g in enumerate((core, other)):
        if step == 1:
            remote(lhsD.at[other], lhsD.at[other], S_DGRAM, sib).wait_recv()
            remote(dsq_v.at[other], dsq_v.at[other], S_DSQ, sib).wait_recv()
        transposed(lhsD, lhsDT, g)
        dsq2 = 2.0 * dsq_v[g][:, 0:1]
        dsk2 = 2.0 * dsq_v[g][:, 1:2]
        for b in range(NB):
            t = pl.ds(b * BLK, BLK)
            q = qkvT[g, :, t]
            k = qkvT[2 + g, :, t]
            dq = nn(lhsD[g][:, :GC], k) + q.astype(F32) * dsq2
            dqkvT[g, :, t] = dq.astype(BF16)
            dk = nn(lhsDT[g][:, :GC], q) + k.astype(F32) * dsk2
            dqkvT[2 + g, :, t] = dk.astype(BF16)
    reduce_next(Pv, Rv, Tv, Iv, S_GWV)
    Pqk[...] = nt(uT[...], dqkvT[pl.ds(0, 4)].reshape(2 * C, NT)).reshape(4, 96, 2 * C)
    reduce_send(Pqk, Rqk, S_GWQK)

    outs = []
    for b in range(NB):
        t = pl.ds(b * BLK, BLK)
        o = oT[:, :, t].reshape(C, BLK)
        y = (xT[:, t].astype(F32) + nn(woT[...], o)).astype(BF16)
        outR[t, :] = transpose_bf16(y)
        if (b + 1) % 4 == 0:
            i = b // 4
            tt = pl.ds(i * 4 * BLK, 4 * BLK)
            d = local(outR.at[tt], out_hbm.at[tt], 10 + i)
            d.start()
            outs.append(d)
    reduce_next(Pqk, Rqk, Tqk, Iqk, S_GWQK)

    ggain = jnp.zeros((C, 128), F32)
    gbias = jnp.zeros((C, 128), F32)
    for b in range(NB):
        t = pl.ds(b * BLK, BLK)
        du = nn(w_v[...], dqkvT[:, :, t].reshape(3 * C, BLK))
        rstd = rstd_v[:, t]
        xhat = (xT[:, t].astype(F32) - mean_v[:, t]) * rstd
        dux = du * xhat
        pg = dux[:, :128]
        pb = du[:, :128]
        for i in range(1, BLK // 128):
            pg = pg + dux[:, 128 * i:128 * i + 128]
            pb = pb + du[:, 128 * i:128 * i + 128]
        if b == 0:
            lnacc[0] = pg
            lnacc[1] = pb
        else:
            lnacc[0] += pg
            lnacc[1] += pb
        dxh = du * wide(gainB)
        m1 = jnp.sum(dxh, axis=0, keepdims=True) * (1.0 / C)
        m2 = jnp.sum(dxh * xhat, axis=0, keepdims=True) * (1.0 / C)
        dx = rstd * (dxh - m1 - xhat * m2)
        gt = (dyT[:, t].astype(F32) + dx).astype(BF16)
        gtR[t, :] = transpose_bf16(gt)
        if (b + 1) % 4 == 0:
            i = b // 4
            tt = pl.ds(i * 4 * BLK, 4 * BLK)
            d = local(gtR.at[tt], gt_hbm.at[tt], 12 + i)
            d.start()
            outs.append(d)
    lnrow = [jnp.sum(lnacc[i].T, axis=0, keepdims=True) for i in range(2)]
    lnsend[...] = jnp.concatenate(lnrow + [jnp.zeros((6, C), F32)], axis=0)
    ln_x = [send(lnsend, lnrecv.at[0], S_LN, sib),
            send(lnsend, lnrecv.at[1], S_LN + 1, cp),
            send(lnsend, lnrecv.at[2], S_LN + 2, dg)]

    row8 = rows((8, 128))
    tl = jnp.zeros((1, 128), F32)
    l1 = lanes((1, 128))
    for g in range(2):
        for h in range(4):
            tl = jnp.where(l1 == 4 * g + h, dsq_v[g, pl.ds(0, 1), 2 + h:3 + h], tl)
    gtemp_ref[...] = tl[:, :8]

    def finish(P, R, I, i):
        remote(P.at[sib], R.at[0], i, sib).wait_recv()
        remote(I, I, i + 2, cp).wait_recv()
        return (P[s] + R[0]) + I[...]

    To2 = finish(Po, Ro, Io, S_GWO)
    Ro[0] = To2
    d = local(Ro.at[0], gwout_hbm, 14)
    d.start()
    outs.append(d)
    Rv[0] = finish(Pv, Rv, Iv, S_GWV)
    d = local(Rv.at[0], gwqkv_hbm.at[:, pl.ds(2 * C, C)], 15)
    d.start()
    outs.append(d)
    for d in ln_x:
        d.wait_recv()
    ln = (lnsend[...] + lnrecv[0]) + (lnrecv[1] + lnrecv[2])
    gg_ref[...] = ln[0:1]
    gb_ref[...] = ln[1:2]
    Rqk[0] = finish(Pqk, Rqk, Iqk, S_GWQK)
    d = local(Rqk.at[0], gwqkv_hbm.at[:, pl.ds(0, 2 * C)], 16)
    d.start()
    outs.append(d)
    for d in pending:
        d.wait_send()
    for d in outs:
        d.wait()


def scratch():
    def v(shape, dtype=F32):
        return pltpu.VMEM(shape, dtype)
    return [
        v((NT, C), BF16), v((NT, C), BF16), v((C, 3 * C), BF16), v((C, C), BF16),
        v((3 * C, C), BF16), v((C, C), BF16),
        v((C, NT), BF16), v((C, NT), BF16), v((C, NT), BF16),
        v((1, NT)), v((1, NT)),
        v((6, GC, NT), BF16), v((2, GC, NT), BF16), v((2, GC, NT), BF16),
        v((6, GC, NT), BF16), v((NT, C), BF16), v((NT, C), BF16),
        v((C, 128)), v((C, 128)), v((2 * C, 128)),
        v((2, GC, 256)), v((2, GC, 256)),
        v((2, 96, 128)), v((3, 96, 128)), v((2, 96, 128)), v((3, 96, 128)),
        v((2, GC, 256), BF16), v((2, GC, 256), BF16), v((2, GC, 256), BF16), v((2, GC, 256), BF16),
        v((2, GC, 128)),
        v((4, 96, C)), v((4, 96, C)), v((4, 96, 2 * C)),
        v((2, 96, C)), v((2, 96, C)), v((2, 96, 2 * C)),
        v((96, C)), v((96, C)), v((96, 2 * C)),
        v((96, C)), v((96, C)), v((96, 2 * C)),
        v((8, C)), v((3, 8, C)), v((2, C, 128)),
        pltpu.SemaphoreType.DMA((N_SEM,)), pltpu.SemaphoreType.DMA((N_SEM,)), pltpu.SemaphoreType.DMA((17,)),
    ]


def solution(mesh):
    row_spec = P(('dp', 'sp'), None)
    part_spec = P('dp')
    full_spec = P()

    def local_step(x_loc, dy_loc, ln_gain, ln_bias, w_qkv, w_out, temperature):
        any_spec = pl.BlockSpec(memory_space=pl.ANY)
        vmem = pl.BlockSpec(memory_space=pltpu.VMEM)
        out = pl.pallas_call(
            body,
            out_shape=(jax.ShapeDtypeStruct((NT, C), BF16), jax.ShapeDtypeStruct((NT, C), BF16),
                       jax.ShapeDtypeStruct((96, 3 * C), F32), jax.ShapeDtypeStruct((96, C), F32),
                       jax.ShapeDtypeStruct((1, C), F32), jax.ShapeDtypeStruct((1, C), F32),
                       jax.ShapeDtypeStruct((1, 8), F32)),
            in_specs=[any_spec, any_spec, vmem, vmem, any_spec, any_spec,
                      pl.BlockSpec(memory_space=pltpu.SMEM)],
            out_specs=(any_spec, any_spec, any_spec, any_spec, vmem, vmem, vmem),
            scratch_shapes=scratch(),
            compiler_params=pltpu.CompilerParams(collective_id=0, has_side_effects=True,
                                                 vmem_limit_bytes=60 * 1024 * 1024),
            name="xca",
        )(x_loc, dy_loc, ln_gain.reshape(1, C), ln_bias.reshape(1, C), w_qkv, w_out, temperature)
        return (out[0], out[1], out[2], out[3], out[4].reshape(C), out[5].reshape(C), out[6].reshape(8))

    return jax.shard_map(local_step, mesh=mesh,
                         in_specs=(row_spec, row_spec, full_spec, full_spec, full_spec, full_spec, full_spec),
                         out_specs=(row_spec, row_spec, row_spec, row_spec, part_spec, part_spec, part_spec),
                         check_vma=False)
```

time: 150 us -> 47.1 us (0.31)
  matrix products: 49.8 us -> 0 us
  waiting for transfers between devices: 44.1 us -> 0 us
  Pallas kernels: 0 us -> 35.1 us
  other arithmetic: 19.8 us -> 2.54 us
  blocking collectives: 15.2 us -> 0 us
  between operations: 14.1 us -> 0.65 us
  local copies, waits for them, and re-layouts: 5.98 us -> 8.53 us
    dot_general x14 -> x0, matrix products: 49.8 us -> none  [the longest x2 8.22 us: project(): jnp.dot(normed, w_qkv, preferred_element_type=jnp.float32)]
    psum x2 -> x0, waiting for transfers between devices: 37.9 us -> none  [the longest x1 20.1 us: local_step(): d_probs = lax.psum(probs_part, 'sp')]
    pallas_call x0 -> x1, Pallas kernels: none -> 35.1 us  [local_step(): pl.pallas_call(body, out_shape=(jax.ShapeDtypeStruct((NT, C), BF16), jax....]
    psum x2 -> x0, blocking collectives: 15.2 us -> none  [the longest x1 8.9 us: local_step(): gram_sum, q_sq, k_sq = lax.psum((gram_part, qsq_part, ksq_part), 'sp')]
    reduce_sum x7 -> x0, other arithmetic: 8.8 us -> none  [the longest x2 3.02 us: layer_norm(): row_var = jnp.mean(centered * centered, axis=-1, keepdims=True)]
    reduce_scatter x2 -> x0, waiting for transfers between devices: 6.08 us -> none  [the longest x1 6.08 us: local_step(): lax.psum_scatter(wqkv_part, 'sp', scatter_dimension=0, tiled=True)]
    convert_element_type x1 -> x0, other arithmetic: 5 us -> none  [local_step(): grad_tokens = (dy_loc.astype(jnp.float32) + d_x).astype(jnp.bfloat16)]
    sub x2 -> x0, other arithmetic: 3.51 us -> none  [attn_probs(): return jax.nn.softmax(value_a11[..., None, None] * cosine, axis=-1)]
  transfers between devices with their start and end apart: 4 -> 0, of which waited for: 3 -> 0; matrix products, arithmetic and copies ran while one was open for 31% -> 0% of each run, Pallas kernels for 0% -> 0%
where the time goes in v1:
time: 47.1 us; the launch traced here: 46.8 us
  Pallas kernels  35.1 us (75%)
  local copies, waits for them, and re-layouts  8.53 us (18%)
  other arithmetic  2.54 us (5%)
  between operations  0.65 us (1%)
    pallas_call x1, Pallas kernels, local_step(): pl.pallas_call(body, out_shape=(jax.ShapeDtypeStruct((NT, C), BF16), jax....  35.1 us
    unnamed x13, local copies, waits for them, and re-layouts  6.04 us
    pallas_call x2, other arithmetic, local_step(): pl.pallas_call(body, out_shape=(jax.ShapeDtypeStruct((NT, C), BF16), jax....  2.54 us
    reshape x1, local copies, waits for them, and re-layouts, local_step(): ln_gain.reshape(1, C)  1.25 us
    reshape x1, local copies, waits for them, and re-layouts, local_step(): ln_bias.reshape(1, C)  1.24 us

profile of v1, /device:TPU:0, one launch (start us, length us, event | category | flops | bytes accessed | tf_op | source)
XLA Modules:
  0.0 46.8 jit_solution(4827285191614230534)
XLA Ops:
  0.6 1.2 %reshape.29.gain_ref = f32[1,384]{1,0:T(1,128)} reshape(f32[384]{0:T(512)} %param.9) | data formatting | bytes 3072 | tf_op jit(solution)/shard_map/reshape | solution.py:435
  1.9 1.2 %reshape.30.bias_ref = f32[1,384]{1,0:T(1,128)} reshape(f32[384]{0:T(512)} %param.10) | data formatting | bytes 3072 | tf_op jit(solution)/shard_map/reshape | solution.py:435
  3.1 35.1 %xca.1 = (bf16[2048,384]{1,0:T(8,128)(2,1)}, bf16[2048,384]{1,0:T(8,128)(2,1)}, f32[96,1152]{1,0:T(8,128)}, f32[96,384]{1,0:T(8,128)}, f32[1,384]{1,0:T(1,128)}, /*index=5*/f32[1,384]{1,0:T(1,128)}, f32[1,8]{1,0:T(1,128)}) custom-call(bf16[2048,384]{1,0:T(8,128)(2,1)} %x_hbm.1, bf16[2048,384]{1,0:T(8,128)(2,1)} %dy_hbm.1, f32[1,384]{1,0:T(1,128)} %reshape.29.gain_ref, ...), custom_call_target="tpu_custom_call" | custom-call | tf_op jit(solution)/shard_map/xca/pallas_call | solution.py:422
  38.3 1.3 %reduce = f32[384]{0:T(512)} reduce(f32[1,384]{1,0:T(1,128)} %get-tuple-element.18, f32[]{:T(128)} %constant), dimensions={0}, to_apply=%get-tuple-element.18.reduce_sub_computation | reduce | bytes 3076 | tf_op jit(solution)/shard_map/xca/pallas_call | solution.py:422
  39.5 1.3 %reduce.1 = f32[384]{0:T(512)} reduce(f32[1,384]{1,0:T(1,128)} %get-tuple-element.19, f32[]{:T(128)} %constant), dimensions={0}, to_apply=%get-tuple-element.19.reduce_sub_computation | reduce | bytes 3076 | tf_op jit(solution)/shard_map/xca/pallas_call | solution.py:422
  40.8 0.0 copy-start
  40.8 2.8 %copy.19 = bf16[2048,384]{1,0:T(8,128)(2,1)} copy(bf16[2048,384]{1,0:T(8,128)(2,1)} %get-tuple-element.28) | data formatting | bytes 3145728
  43.6 0.0 copy-done
  43.6 0.0 copy-start.1
  43.6 0.0 copy-start.2
  43.6 0.0 copy-start.3
  43.6 1.1 %copy.20 = bf16[2048,384]{1,0:T(8,128)(2,1)} copy(bf16[2048,384]{1,0:T(8,128)(2,1)S(1)} %copy-done) | data formatting | bytes 3145728
  44.8 0.1 copy-done.1
  44.9 0.8 %copy.21 = f32[96,1152]{1,0:T(8,128)} copy(f32[96,1152]{1,0:T(8,128)S(1)} %copy-done.1) | data formatting | bytes 884736
  45.7 0.0 copy-done.2
  45.7 0.7 %copy.22 = f32[96,384]{1,0:T(8,128)} copy(f32[96,384]{1,0:T(8,128)S(1)} %copy-done.2) | data formatting | bytes 294912
  46.3 0.0 copy-done.3
  46.3 0.5 %copy.23 = f32[8]{0:T(128)} copy(f32[8]{0:T(128)S(1)} %bitcast.1) | data formatting | bytes 64
Async XLA Ops:
  40.8 2.8 %copy-start = (bf16[2048,384]{1,0:T(8,128)(2,1)S(1)}, bf16[2048,384]{1,0:T(8,128)(2,1)}, u32[]{:S(2)}) copy-start(bf16[2048,384]{1,0:T(8,128)(2,1)} %get-tuple-element.29) | copy-start | bytes 4718596
  43.6 1.3 %copy-start.1 = (f32[96,1152]{1,0:T(8,128)S(1)}, f32[96,1152]{1,0:T(8,128)}, u32[]{:S(2)}) copy-start(f32[96,1152]{1,0:T(8,128)} %get-tuple-element.30) | copy-start | bytes 1327108
  43.6 2.0 %copy-start.2 = (f32[96,384]{1,0:T(8,128)S(1)}, f32[96,384]{1,0:T(8,128)}, u32[]{:S(2)}) copy-start(f32[96,384]{1,0:T(8,128)} %get-tuple-element.31) | copy-start | bytes 442372
  43.6 2.7 %copy-start.3 = (f32[1,8]{1,0:T(1,128)S(1)}, f32[1,8]{1,0:T(1,128)}, u32[]{:S(2)}) copy-start(f32[1,8]{1,0:T(1,128)} %get-tuple-element.20) | copy-start | bytes 100

commit v2 on v1

--- a/solution.py
+++ b/solution.py
@@ -99,12 +99,12 @@
     return jnp.concatenate(parts, axis=0)
 
 
-def body(x_hbm, dy_hbm, gain_ref, bias_ref, wqkv_hbm, wout_hbm, temp_ref,
-         out_hbm, gt_hbm, gwqkv_hbm, gwout_hbm, gg_ref, gb_ref, gtemp_ref,
-         x_v, dy_v, w_v, wo_v, wT, woT, xT, dyT, uT, mean_v, rstd_v, qkvT, doT, oT, dqkvT, outR, gtR,
+def body(x_hbm, dy_hbm, gain_hbm, bias_hbm, wqkv_hbm, wout_hbm, temp_hbm,
+         outR, gtR, gwqkv_o, gwout_o, small_o,
+         x_v, dy_v, w_v, wo_v, wT, woT, xT, dyT, uT, mean_v, rstd_v, qkvT, doT, oT, dqkvT,
          gainB, biasB, ssq, gacc, dacc, gsend, grecv, dsend, drecv, lhsA, lhsAT, lhsD, lhsDT, dsq_v,
          Po, Pv, Pqk, Ro, Rv, Rqk, To, Tv, Tqk, Io, Iv, Iqk, lnsend, lnrecv, lnacc,
-         ssem, rsem, dsem):
+         gain_ref, bias_ref, temp_ref, ssem, rsem, dsem):
     s = lax.axis_index("sp")
     chip, core = s // 2, s % 2
     sib = chip * 2 + (1 - core)
@@ -129,13 +129,19 @@
     in_wo = local(wout_hbm, wo_v, 1)
     in_x = [local(x_hbm.at[pl.ds(i * xr, xr)], x_v.at[pl.ds(i * xr, xr)], 2 + i) for i in range(nx)]
     in_dy = [local(dy_hbm.at[pl.ds(i * xr, xr)], dy_v.at[pl.ds(i * xr, xr)], 6 + i) for i in range(nx)]
+    in_small = [local(gain_hbm, gain_ref, 10), local(bias_hbm, bias_ref, 11), local(temp_hbm, temp_ref, 12)]
     in_x[0].start()
+    in_small[0].start()
+    in_small[1].start()
     in_w.start()
+    in_small[2].start()
     for d in in_x[1:] + [in_wo] + in_dy:
         d.start()
 
-    gainB[...] = jnp.broadcast_to(gain_ref[...], (128, C)).T
-    biasB[...] = jnp.broadcast_to(bias_ref[...], (128, C)).T
+    in_small[0].wait()
+    in_small[1].wait()
+    gainB[...] = jnp.broadcast_to(gain_ref[...].reshape(1, C), (128, C)).T
+    biasB[...] = jnp.broadcast_to(bias_ref[...].reshape(1, C), (128, C)).T
     gacc[...] = jnp.zeros(gacc.shape, F32)
     dacc[...] = jnp.zeros(dacc.shape, F32)
 
@@ -209,6 +215,7 @@
                send(dsend.at[other], drecv.at[2], S_DPROB + 2, dg),
                send(dsend.at[other], drecv.at[0], S_DPROB, sib)]
 
+    in_small[2].wait()
     for d in gram_x:
         d.wait_recv()
     lane = lanes((GC, 128))
@@ -299,18 +306,11 @@
     Pqk[...] = nt(uT[...], dqkvT[pl.ds(0, 4)].reshape(2 * C, NT)).reshape(4, 96, 2 * C)
     reduce_send(Pqk, Rqk, S_GWQK)
 
-    outs = []
     for b in range(NB):
         t = pl.ds(b * BLK, BLK)
         o = oT[:, :, t].reshape(C, BLK)
         y = (xT[:, t].astype(F32) + nn(woT[...], o)).astype(BF16)
         outR[t, :] = transpose_bf16(y)
-        if (b + 1) % 4 == 0:
-            i = b // 4
-            tt = pl.ds(i * 4 * BLK, 4 * BLK)
-            d = local(outR.at[tt], out_hbm.at[tt], 10 + i)
-            d.start()
-            outs.append(d)
     reduce_next(Pqk, Rqk, Tqk, Iqk, S_GWQK)
 
     ggain = jnp.zeros((C, 128), F32)
@@ -338,12 +338,6 @@
         dx = rstd * (dxh - m1 - xhat * m2)
         gt = (dyT[:, t].astype(F32) + dx).astype(BF16)
         gtR[t, :] = transpose_bf16(gt)
-        if (b + 1) % 4 == 0:
-            i = b // 4
-            tt = pl.ds(i * 4 * BLK, 4 * BLK)
-            d = local(gtR.at[tt], gt_hbm.at[tt], 12 + i)
-            d.start()
-            outs.append(d)
     lnrow = [jnp.sum(lnacc[i].T, axis=0, keepdims=True) for i in range(2)]
     lnsend[...] = jnp.concatenate(lnrow + [jnp.zeros((6, C), F32)], axis=0)
     ln_x = [send(lnsend, lnrecv.at[0], S_LN, sib),
@@ -356,35 +350,33 @@
     for g in range(2):
         for h in range(4):
             tl = jnp.where(l1 == 4 * g + h, dsq_v[g, pl.ds(0, 1), 2 + h:3 + h], tl)
-    gtemp_ref[...] = tl[:, :8]
+    small_o[pl.ds(2, 1), pl.ds(0, 128)] = tl
 
     def finish(P, R, I, i):
         remote(P.at[sib], R.at[0], i, sib).wait_recv()
         remote(I, I, i + 2, cp).wait_recv()
         return (P[s] + R[0]) + I[...]
 
-    To2 = finish(Po, Ro, Io, S_GWO)
-    Ro[0] = To2
-    d = local(Ro.at[0], gwout_hbm, 14)
-    d.start()
-    outs.append(d)
-    Rv[0] = finish(Pv, Rv, Iv, S_GWV)
-    d = local(Rv.at[0], gwqkv_hbm.at[:, pl.ds(2 * C, C)], 15)
-    d.start()
-    outs.append(d)
+    gwout_o[...] = finish(Po, Ro, Io, S_GWO)
+    gwqkv_o[:, pl.ds(2 * C, C)] = finish(Pv, Rv, Iv, S_GWV)
     for d in ln_x:
         d.wait_recv()
-    ln = (lnsend[...] + lnrecv[0]) + (lnrecv[1] + lnrecv[2])
-    gg_ref[...] = ln[0:1]
-    gb_ref[...] = ln[1:2]
-    Rqk[0] = finish(Pqk, Rqk, Iqk, S_GWQK)
-    d = local(Rqk.at[0], gwqkv_hbm.at[:, pl.ds(0, 2 * C)], 16)
-    d.start()
-    outs.append(d)
+    small_o[pl.ds(0, 2), :] = ((lnsend[...] + lnrecv[0]) + (lnrecv[1] + lnrecv[2]))[0:2]
+    gwqkv_o[:, pl.ds(0, 2 * C)] = finish(Pqk, Rqk, Iqk, S_GWQK)
     for d in pending:
         d.wait_send()
-    for d in outs:
-        d.wait()
+
+
+def emit(out_v, gt_v, gwqkv_v, gwout_v, small_v, out_hbm, gt_hbm, gwqkv_hbm, gwout_hbm, gg_ref, gb_ref, gtemp_ref, sem):
+    copies = [pltpu.make_async_copy(a, b, sem.at[i]) for i, (a, b) in enumerate(
+        ((out_v, out_hbm), (gt_v, gt_hbm), (gwqkv_v, gwqkv_hbm), (gwout_v, gwout_hbm)))]
+    for c in copies:
+        c.start()
+    gg_ref[...] = small_v[0, :]
+    gb_ref[...] = small_v[1, :]
+    gtemp_ref[...] = small_v[2, :8]
+    for c in copies:
+        c.wait()
 
 
 def scratch():
@@ -396,7 +388,7 @@
         v((C, NT), BF16), v((C, NT), BF16), v((C, NT), BF16),
         v((1, NT)), v((1, NT)),
         v((6, GC, NT), BF16), v((2, GC, NT), BF16), v((2, GC, NT), BF16),
-        v((6, GC, NT), BF16), v((NT, C), BF16), v((NT, C), BF16),
+        v((6, GC, NT), BF16),
         v((C, 128)), v((C, 128)), v((2 * C, 128)),
         v((2, GC, 256)), v((2, GC, 256)),
         v((2, 96, 128)), v((3, 96, 128)), v((2, 96, 128)), v((3, 96, 128)),
@@ -407,7 +399,8 @@
         v((96, C)), v((96, C)), v((96, 2 * C)),
         v((96, C)), v((96, C)), v((96, 2 * C)),
         v((8, C)), v((3, 8, C)), v((2, C, 128)),
-        pltpu.SemaphoreType.DMA((N_SEM,)), pltpu.SemaphoreType.DMA((N_SEM,)), pltpu.SemaphoreType.DMA((17,)),
+        v((C,)), v((C,)), pltpu.SMEM((8,), F32),
+        pltpu.SemaphoreType.DMA((N_SEM,)), pltpu.SemaphoreType.DMA((N_SEM,)), pltpu.SemaphoreType.DMA((13,)),
     ]
 
 
@@ -417,23 +410,34 @@
     full_spec = P()
 
     def local_step(x_loc, dy_loc, ln_gain, ln_bias, w_qkv, w_out, temperature):
-        any_spec = pl.BlockSpec(memory_space=pl.ANY)
+        hbm = pl.BlockSpec(memory_space=pltpu.HBM)
         vmem = pl.BlockSpec(memory_space=pltpu.VMEM)
+        args = [pltpu.with_memory_space_constraint(a, pltpu.HBM)
+                for a in (x_loc, dy_loc, ln_gain, ln_bias, w_qkv, w_out, temperature)]
         out = pl.pallas_call(
             body,
+            out_shape=(pltpu.VMEM((NT, C), BF16), pltpu.VMEM((NT, C), BF16), pltpu.VMEM((96, 3 * C), F32),
+                       pltpu.VMEM((96, C), F32), pltpu.VMEM((8, C), F32)),
+            in_specs=[hbm] * 7,
+            out_specs=(vmem,) * 5,
+            scratch_shapes=scratch(),
+            compiler_params=pltpu.CompilerParams(collective_id=0, has_side_effects=True,
+                                                 vmem_limit_bytes=48 * 1024 * 1024),
+            name="xca",
+        )(*args)
+        out = [pltpu.with_memory_space_constraint(o, pltpu.VMEM) for o in out]
+        return pl.pallas_call(
+            emit,
             out_shape=(jax.ShapeDtypeStruct((NT, C), BF16), jax.ShapeDtypeStruct((NT, C), BF16),
                        jax.ShapeDtypeStruct((96, 3 * C), F32), jax.ShapeDtypeStruct((96, C), F32),
-                       jax.ShapeDtypeStruct((1, C), F32), jax.ShapeDtypeStruct((1, C), F32),
-                       jax.ShapeDtypeStruct((1, 8), F32)),
-            in_specs=[any_spec, any_spec, vmem, vmem, any_spec, any_spec,
-                      pl.BlockSpec(memory_space=pltpu.SMEM)],
-            out_specs=(any_spec, any_spec, any_spec, any_spec, vmem, vmem, vmem),
-            scratch_shapes=scratch(),
-            compiler_params=pltpu.CompilerParams(collective_id=0, has_side_effects=True,
-                                                 vmem_limit_bytes=60 * 1024 * 1024),
-            name="xca",
-        )(x_loc, dy_loc, ln_gain.reshape(1, C), ln_bias.reshape(1, C), w_qkv, w_out, temperature)
-        return (out[0], out[1], out[2], out[3], out[4].reshape(C), out[5].reshape(C), out[6].reshape(8))
+                       jax.ShapeDtypeStruct((C,), F32), jax.ShapeDtypeStruct((C,), F32),
+                       jax.ShapeDtypeStruct((8,), F32)),
+            in_specs=[vmem] * 5,
+            out_specs=(hbm,) * 4 + (vmem,) * 3,
+            scratch_shapes=[pltpu.SemaphoreType.DMA((4,))],
+            compiler_params=pltpu.CompilerParams(vmem_limit_bytes=12 * 1024 * 1024),
+            name="emit",
+        )(*out)
 
     return jax.shard_map(local_step, mesh=mesh,
                          in_specs=(row_spec, row_spec, full_spec, full_spec, full_spec, full_spec, full_spec),

time: 47.1 us -> 36.4 us (0.77)
  local copies, waits for them, and re-layouts: 8.53 us -> 0 us
  other arithmetic: 2.54 us -> 0 us
    unnamed x13 -> x0, local copies, waits for them, and re-layouts: 6.04 us -> none
    pallas_call x2 -> x0, other arithmetic: 2.54 us -> none  [local_step(): pl.pallas_call(body, out_shape=(jax.ShapeDtypeStruct((NT, C), BF16), jax....]
    reshape x2 -> x0, local copies, waits for them, and re-layouts: 2.49 us -> none  [the longest x1 1.25 us: local_step(): ln_gain.reshape(1, C)]
    pallas_call x1 -> x2, Pallas kernels: 35.1 us -> 35.5 us  [the longest x1 33.1 us: local_step(): pl.pallas_call(body, out_shape=(pltpu.VMEM((NT, C), BF16), pltpu.VMEM((NT...]
where the time goes in v2:
time: 36.4 us; the launch traced here: 36.3 us
  Pallas kernels  35.5 us (98%)
  between operations  0.8 us (2%)
    pallas_call x1, Pallas kernels, local_step(): pl.pallas_call(body, out_shape=(pltpu.VMEM((NT, C), BF16), pltpu.VMEM((NT...  33.1 us
    pallas_call x1, Pallas kernels, local_step(): pl.pallas_call(emit, out_shape=(jax.ShapeDtypeStruct((NT, C), BF16), jax....  2.45 us

profile of v2, /device:TPU:0, one launch (start us, length us, event | category | flops | bytes accessed | tf_op | source)
XLA Modules:
  0.0 36.3 jit_solution(16916486250736759232)
XLA Ops:
  0.6 33.1 %xca.1 = (bf16[2048,384]{1,0:T(8,128)(2,1)S(1)}, bf16[2048,384]{1,0:T(8,128)(2,1)S(1)}, f32[96,1152]{1,0:T(8,128)S(1)}, f32[96,384]{1,0:T(8,128)S(1)}, f32[8,384]{1,0:T(8,128)S(1)}) custom-call(bf16[2048,384]{1,0:T(8,128)(2,1)} %x_hbm.1, bf16[2048,384]{1,0:T(8,128)(2,1)} %dy_hbm.1, f32[384]{0:T(512)} %gain_hbm.1, f32[384]{0:T(512)} %bias_hbm.1, ...), custom_call_target="tpu_custom_call" | custom-call | tf_op jit(solution)/shard_map/xca/pallas_call | solution.py:417
  33.7 2.4 %emit.1 = (bf16[2048,384]{1,0:T(8,128)(2,1)}, bf16[2048,384]{1,0:T(8,128)(2,1)}, f32[96,1152]{1,0:T(8,128)}, f32[96,384]{1,0:T(8,128)}, f32[384]{0:T(512)}, /*index=5*/f32[384]{0:T(512)}, f32[8]{0:T(128)}) custom-call(bf16[2048,384]{1,0:T(8,128)(2,1)S(1)} %get-tuple-element.12.out_v, bf16[2048,384]{1,0:T(8,128)(2,1)S(1)} %get-tuple-element.13.gt_v, ...), custom_call_target="tpu_custom_call" | custom-call | tf_op jit(solution)/shard_map/emit/pallas_call | solution.py:429
